TPU v7x, 32 devices: a whole 2x2x4 slice. The times are simulated.
32 devices in a mesh: dp: 4 (over z), expert: 2 (over x), tensor: 4 (over y, core).
Axes of the slice: x: 2, y: 2, z: 4, core: 2. Of those that a mesh axis runs over, the one named last changes fastest.
Arguments:
- tokens: bfloat16 [256, 4096], P(('dp', 'expert', 'tensor')), may hold values from -6 to 6
- out_grad: bfloat16 [256, 4096], P(('dp', 'expert', 'tensor')), may hold values from -4 to 4
- route_probs: float32 [256, 2], P(('dp', 'expert')), may hold values from 0.2 to 1
- expert_ids: int32 [256, 2], P(('dp', 'expert')), may hold values from 0 to 7, as said below
- slot_index: int32 [256, 2], P(('dp', 'expert')), may hold values from 0 to 10, as said below
- w_gate: bfloat16 [8, 4096, 7168], P('expert', 'dp', 'tensor'), may hold values from -0.09375 to 0.09375
- w_up: bfloat16 [8, 4096, 7168], P('expert', 'dp', 'tensor'), may hold values from -0.09375 to 0.09375
- w_down: bfloat16 [8, 7168, 4096], P('expert', 'tensor', 'dp'), may hold values from -0.0625 to 0.0625
Outputs:
- token_grad: bfloat16 [256, 4096], P(('dp', 'expert', 'tensor'))
- grad_gate: bfloat16 [8, 4096, 7168], P('expert', 'dp', 'tensor')
- grad_up: bfloat16 [8, 4096, 7168], P('expert', 'dp', 'tensor')
- grad_down: bfloat16 [8, 7168, 4096], P('expert', 'tensor', 'dp')
Inputs may be any that keep to these rules, and one draw needn't show every extreme that they name: `expert_ids`: the 2 entries of a token are different experts. slot_index[t, k] counts the earlier routes to expert_ids[t, k] within the token's routing block of 32 rows, in order of tokens and then of routes; the value 10 marks a route past the capacity, which is dropped (a count of 10 or more is given as 10). In every draw some expert is filled to 10 slots in every block.
All inputs are finite; a program needn't handle non-finite values.
Results may differ from a plain program's by a relative error of at most 0.011.
Values may be sent and summed in bfloat16 or wider, within the bound.
A program may use at most 192 MiB of HBM per device.

v0:
```python
import jax
import jax.numpy as jnp
from jax import lax
from jax.sharding import PartitionSpec as P

EXPERTS = 8
TOP = 2


def swiglu_back(pre_gate, pre_up, grad_hidden):
    sigmoid_gate = jax.nn.sigmoid(pre_gate)
    silu_gate = pre_gate * sigmoid_gate
    hidden = (silu_gate * pre_up).astype(jnp.bfloat16)
    up_delta = (grad_hidden * silu_gate).astype(jnp.bfloat16)
    gate_delta = (
        grad_hidden * pre_up * sigmoid_gate * (1.0 + pre_gate * (1.0 - sigmoid_gate))
    ).astype(jnp.bfloat16)
    return (hidden, gate_delta, up_delta)


def shards(tokens, out_grad, route_probs, expert_ids, slot_index, w_gate, w_up, w_down):
    f32, bf16 = jnp.float32, jnp.bfloat16
    dp, groups, parts = (lax.axis_size(a) for a in ("dp", "expert", "tensor"))
    held, model_width = tokens.shape
    block_rows = held * parts
    blocks = dp * groups
    slice_width = model_width // dp
    count = blocks * block_rows
    capacity = 5 * block_rows * TOP // (4 * EXPERTS)
    local_experts = w_gate.shape[0]
    rows = blocks * capacity

    route = jnp.concatenate(
        [route_probs, expert_ids.astype(f32), slot_index.astype(f32)], axis=1
    )
    route = lax.all_gather(route, ("dp", "expert"), axis=0, tiled=True)
    both = jnp.stack([tokens, out_grad])
    both = lax.all_to_all(both, "dp", split_axis=2, concat_axis=1, tiled=True)
    both = lax.all_gather(both, ("expert", "tensor"), axis=1, tiled=True)
    x_all, dy_all = both[0], both[1]
    route = route.reshape(dp, groups, parts, held, 3 * TOP)
    route = route.transpose(1, 2, 0, 3, 4).reshape(count, 3 * TOP)
    probs = route[:, :TOP]
    ids = route[:, TOP : 2 * TOP].astype(jnp.int32)
    slots = route[:, 2 * TOP :].astype(jnp.int32)
    order = jnp.arange(count, dtype=jnp.int32)
    block = (order // held % dp) * groups + order // (held * dp * parts)
    local = ids - lax.axis_index("expert") * local_experts
    keep = (slots < capacity) & (local >= 0) & (local < local_experts)
    target = jnp.where(keep, local * rows + block[:, None] * capacity + slots, -1)
    places = jnp.arange(local_experts * rows, dtype=jnp.int32)
    tables = [(places[:, None] == target[None, :, k]).astype(bf16) for k in range(TOP)]
    table_sum = tables[0] + tables[1]
    dy_wide = dy_all.astype(f32)
    scaled = jnp.concatenate([(probs[:, k : k + 1] * dy_wide).astype(bf16) for k in range(TOP)])
    x = jnp.dot(table_sum, x_all, preferred_element_type=f32).astype(bf16)
    g = jnp.dot(jnp.concatenate(tables, 1), scaled, preferred_element_type=f32).astype(bf16)
    x = x.reshape(local_experts, rows, slice_width)
    g = g.reshape(local_experts, rows, slice_width)

    def summed(spec, left, right):
        part = jnp.einsum(spec, left, right, preferred_element_type=f32).astype(bf16)
        part = part.reshape(local_experts * rows, part.shape[2])
        return lax.psum_scatter(part, "dp", scatter_dimension=0, tiled=True).astype(f32)

    pre_gate = summed("lnd,ldf->lnf", x, w_gate)
    pre_up = summed("lnd,ldf->lnf", x, w_up)
    grad_hidden = summed("lnd,lfd->lnf", g, w_down)

    def spread(part):
        whole = lax.all_gather(part, "dp", axis=0, tiled=True)
        return whole.reshape(local_experts, rows, whole.shape[1])

    hidden, gate_delta, up_delta = swiglu_back(pre_gate, pre_up, grad_hidden)
    gate_delta = spread(gate_delta)
    up_delta = spread(up_delta)
    hidden = spread(hidden)
    row_grad = jnp.einsum("lnf,ldf->lnd", gate_delta, w_gate, preferred_element_type=f32)
    row_grad = row_grad + jnp.einsum("lnf,ldf->lnd", up_delta, w_up, preferred_element_type=f32)
    row_grad = row_grad.astype(bf16).reshape(local_experts * rows, slice_width)
    token_part = lax.dot_general(
        table_sum, row_grad, (((0,), (0,)), ((), ())), preferred_element_type=f32
    ).astype(bf16)
    token_part = lax.psum_scatter(
        token_part, ("expert", "tensor"), scatter_dimension=0, tiled=True
    )
    token_grad = lax.all_to_all(token_part, "dp", split_axis=0, concat_axis=1, tiled=True)
    grad_gate = jnp.einsum("lnd,lnf->ldf", x, gate_delta, preferred_element_type=f32)
    grad_up = jnp.einsum("lnd,lnf->ldf", x, up_delta, preferred_element_type=f32)
    grad_down = jnp.einsum("lnf,lnd->lfd", hidden, g, preferred_element_type=f32)
    return (
        token_grad.astype(bf16),
        grad_gate.astype(bf16),
        grad_up.astype(bf16),
        grad_down.astype(bf16),
    )


def solution(mesh):
    placed = (
        P(("dp", "expert", "tensor"), None),
        P(("dp", "expert", "tensor"), None),
        P(("dp", "expert"), None),
        P(("dp", "expert"), None),
        P(("dp", "expert"), None),
        P("expert", "dp", "tensor"),
        P("expert", "dp", "tensor"),
        P("expert", "tensor", "dp"),
    )
    return jax.shard_map(
        shards,
        mesh=mesh,
        in_specs=placed,
        out_specs=(
            P(("dp", "expert", "tensor"), None),
            P("expert", "dp", "tensor"),
            P("expert", "dp", "tensor"),
            P("expert", "tensor", "dp"),
        ),
        check_vma=False,
    )
```

profile of v0, /device:TPU:0, one launch (start us, length us, event | category | flops | bytes accessed | tf_op | source)
XLA Modules:
  0.0 316.4 jit_solution(10031762522473105389)
XLA Ops:
  8.1 2.8 copy.23
  10.9 2.2 reshape.99
  13.1 12.2 %all_to_all.37 = bf16[4,2,8192]{2,1,0:T(2,128)(2,1)S(1)} all-to-all(bf16[4,2,8192]{2,1,0:T(2,128)(2,1)S(1)} %reshape.99), channel_id=1, replica_groups=mesh['dp'=4,'expert'=2,'tensor'=4] {'dp'}, dimensions={0} | all-to-all | bytes 262144 | tf_op jit(solution)/shard_map/all_to_all | solution.py:38
  25.3 2.4 reshape.100
  27.8 1.3 copy.26
  30.0 30.6 %all-gather = f32[8,32,6]{1,2,0:T(8,128)S(1)} all-gather(f32[1,32,6]{1,2,0:T(8,128)S(1)} %maximum_bitcast_fusion), channel_id=1, replica_groups=mesh['dp'=4,'expert'=2,'tensor'=4] {'dp','expert'}, dimensions={0}, use_global_device_ids=true | all-gather | bytes 6912 | tf_op jit(solution)/shard_map/all_gather | solution.py:36
  62.9 10.8 %convolution_convert_fusion.5 = bf16[4,80,1792]{2,1,0:T(8,128)(2,1)} fusion(bf16[4,80,1024]{2,1,0:T(8,128)(2,1)S(1)} %bitcast.71, bf16[4,1792,1024]{2,1,0:T(8,128)(2,1)} %param.15), kind=kOutput, calls=%fused_computation.5 | convolution fusion | flops 1174978560 | bytes 16482304 | tf_op jit(solution)/shard_map/lnd,lfd->lnf/dot_general | solution.py:62
  74.1 8.9 %convolution_convert_fusion.3 = bf16[4,80,1792]{2,1,0:T(8,128)(2,1)} fusion(bf16[4,80,1024]{2,1,0:T(8,128)(2,1)S(1)} %bitcast.60, bf16[4,1024,1792]{2,1,0:T(8,128)(2,1)} %param.13), kind=kOutput, calls=%fused_computation.3 | convolution fusion | flops 1174978560 | bytes 16482304 | tf_op jit(solution)/shard_map/lnd,ldf->lnf/dot_general | solution.py:62
  83.1 8.8 %convolution_convert_fusion.4 = bf16[4,80,1792]{2,1,0:T(8,128)(2,1)} fusion(bf16[4,80,1024]{2,1,0:T(8,128)(2,1)S(1)} %bitcast.61, bf16[4,1024,1792]{2,1,0:T(8,128)(2,1)} %param.14), kind=kOutput, calls=%fused_computation.4 | convolution fusion | flops 1174978560 | bytes 16482304 | tf_op jit(solution)/shard_map/lnd,ldf->lnf/dot_general | solution.py:62
  92.0 9.8 %reduce-scatter.5.cloned.1.call-done = bf16[80,1792]{1,0:T(8,128)(2,1)} async-done(((bf16[320,1792]{1,0:T(8,128)(2,1)}), bf16[80,1792]{1,0:T(8,128)(2,1)}) %reduce-scatter.5.cloned.1.call-update) | async-done | bytes 286736 | tf_op jit(solution)/shard_map/reduce_scatter | solution.py:64
  101.8 30.3 %reduce-scatter.9.cloned.1.call-done = bf16[80,1792]{1,0:T(8,128)(2,1)} async-done(((bf16[320,1792]{1,0:T(8,128)(2,1)}), bf16[80,1792]{1,0:T(8,128)(2,1)}) %reduce-scatter.9.cloned.1.call-update) | async-done | bytes 286736 | tf_op jit(solution)/shard_map/reduce_scatter | solution.py:64
  132.0 30.2 %reduce-scatter.7.cloned.1.call-done = bf16[80,1792]{1,0:T(8,128)(2,1)} async-done(((bf16[320,1792]{1,0:T(8,128)(2,1)}), bf16[80,1792]{1,0:T(8,128)(2,1)}) %reduce-scatter.7.cloned.1.call-update) | async-done | bytes 286736 | tf_op jit(solution)/shard_map/reduce_scatter | solution.py:64
  162.2 2.3 fusion.10
  165.4 27.5 %all-gather.8.cloned.1.call-done = bf16[320,1792]{1,0:T(8,128)(2,1)} async-done(((bf16[80,1792]{1,0:T(8,128)(2,1)}), bf16[320,1792]{1,0:T(8,128)(2,1)}) %all-gather.8.cloned.1.call-update) | async-done | bytes 1146896 | tf_op jit(solution)/shard_map/all_gather | solution.py:71
  192.9 10.0 %fusion.33 = f32[4,80,1024]{2,1,0:T(8,128)S(1)} fusion(bf16[4,80,1792]{2,1,0:T(8,128)(2,1)} %bitcast.64, bf16[4,1024,1792]{2,1,0:T(8,128)(2,1)} %param.13), kind=kOutput, calls=%fused_computation.67 | convolution fusion | flops 1174405120 | bytes 17137664 | tf_op jit(solution)/shard_map/lnf,ldf->lnd/dot_general | solution.py:78
  202.9 21.0 %all-gather.10.cloned.1.call-done = bf16[320,1792]{1,0:T(8,128)(2,1)} async-done(((bf16[80,1792]{1,0:T(8,128)(2,1)}), bf16[320,1792]{1,0:T(8,128)(2,1)}) %all-gather.10.cloned.1.call-update) | async-done | bytes 1146896 | tf_op jit(solution)/shard_map/all_gather | solution.py:71
  223.9 10.0 %fusion = bf16[4,80,1024]{2,1,0:T(8,128)(2,1)S(1)} fusion(f32[4,80,1024]{2,1,0:T(8,128)S(1)} %fusion.33, bf16[4,80,1792]{2,1,0:T(8,128)(2,1)} %bitcast.66, bf16[4,1024,1792]{2,1,0:T(8,128)(2,1)} %param.14), kind=kOutput, calls=%fused_computation.7 | convolution fusion | flops 1175060480 | bytes 17793024 | tf_op jit(solution)/shard_map/lnf,ldf->lnd/dot_general | solution.py:79
  233.9 1.3 convolution_convert_fusion.8
  236.0 7.6 %convolution_convert_fusion.1 = bf16[4,1024,1792]{2,1,0:T(8,128)(2,1)} fusion(bf16[4,80,1024]{2,1,0:T(8,128)(2,1)S(1)} %bitcast.62, bf16[4,80,1792]{2,1,0:T(8,128)(2,1)S(1)} %bitcast.67), kind=kOutput, calls=%fused_computation.1 | convolution fusion | flops 1181745152 | bytes 16482304 | tf_op jit(solution)/shard_map/lnd,lnf->ldf/dot_general | solution.py:89
  243.6 7.6 %convolution_convert_fusion.2 = bf16[4,1024,1792]{2,1,0:T(8,128)(2,1)} fusion(bf16[4,80,1024]{2,1,0:T(8,128)(2,1)S(1)} %bitcast.63, bf16[4,80,1792]{2,1,0:T(8,128)(2,1)S(1)} %bitcast.65), kind=kOutput, calls=%fused_computation.2 | convolution fusion | flops 1181745152 | bytes 16482304 | tf_op jit(solution)/shard_map/lnd,lnf->ldf/dot_general | solution.py:88
  251.2 17.7 %reduce-scatter.11.cloned.1.call-done = bf16[32,1024]{1,0:T(8,128)(2,1)} async-done(((bf16[256,1024]{1,0:T(8,128)(2,1)}), bf16[32,1024]{1,0:T(8,128)(2,1)}) %reduce-scatter.11.cloned.1.call-update) | async-done | bytes 65552 | tf_op jit(solution)/shard_map/reduce_scatter | solution.py:84
  268.9 4.6 %all-to-all-start.1 = ((bf16[4,8,1024]{2,1,0:T(8,128)(2,1)}), bf16[4,8,1024]{2,1,0:T(8,128)(2,1)S(1)}, u32[]{:S(2)}, u32[]{:S(2)}) async-start(bf16[4,8,1024]{2,1,0:T(8,128)(2,1)} %bitcast.81), calls=%async_computation.5 | async-start | bytes 131072 | tf_op jit(solution)/shard_map/all_to_all | solution.py:87
  273.5 26.6 %all-gather.12.cloned.1.call-done = bf16[320,1792]{1,0:T(8,128)(2,1)} async-done(((bf16[80,1792]{1,0:T(8,128)(2,1)}), bf16[320,1792]{1,0:T(8,128)(2,1)}) %all-gather.12.cloned.1.call-update) | async-done | bytes 1146896 | tf_op jit(solution)/shard_map/all_gather | solution.py:71
  300.1 8.8 %convolution_convert_fusion = bf16[4,1792,1024]{2,1,0:T(8,128)(2,1)} fusion(bf16[4,80,1792]{2,1,0:T(8,128)(2,1)} %bitcast.75, bf16[4,80,1024]{2,1,0:T(8,128)(2,1)S(1)} %bitcast.72), kind=kOutput, calls=%fused_computation | convolution fusion | flops 1181745152 | bytes 16482304 | tf_op jit(solution)/shard_map/lnf,lnd->lfd/dot_general | solution.py:90
  (48 shorter events, 6.6 us)
Async XLA Ops:
  7.2 53.9 %all-gather.6.cloned.1.call-start = ((), (), s32[]{:S(2)}) async-start(), calls=%async_computation.6 | async-start | bytes 1179648 | tf_op jit(solution)/shard_map/all_gather | solution.py:39
  25.3 4.6 %copy-start.4 = (s32[32,2]{0,1:T(2,128)S(1)}, s32[32,2]{0,1:T(2,128)}, u32[]{:S(2)}) copy-start(s32[32,2]{0,1:T(2,128)} %param.11) | copy-start | bytes 772
  25.3 4.6 %copy-start.5 = (s32[32,2]{0,1:T(2,128)S(1)}, s32[32,2]{0,1:T(2,128)}, u32[]{:S(2)}) copy-start(s32[32,2]{0,1:T(2,128)} %param.12) | copy-start | bytes 772
  25.3 4.6 %copy-start.3 = (f32[32,2]{0,1:T(2,128)S(1)}, f32[32,2]{0,1:T(2,128)}, u32[]{:S(2)}) copy-start(f32[32,2]{0,1:T(2,128)} %param.10) | copy-start | bytes 772
  29.8 71.9 %reduce-scatter.5.cloned.1.call-start = ((), (), s32[]{:S(2)}) async-start(), calls=%async_computation.7 | async-start | bytes 1433600 | tf_op jit(solution)/shard_map/reduce_scatter | solution.py:64
  62.8 10.9 %copy-start.2 = (bf16[2,256,1024]{2,1,0:T(8,128)(2,1)S(1)}, bf16[2,256,1024]{2,1,0:T(8,128)(2,1)}, u32[]{:S(2)}) copy-start(bf16[2,256,1024]{2,1,0:T(8,128)(2,1)} %all-gather.6.cloned.1.call-done) | copy-start | bytes 3145732
  73.7 58.4 %reduce-scatter.9.cloned.1.call-start = ((), (), s32[]{:S(2)}) async-start(), calls=%async_computation.9 | async-start | bytes 1433600 | tf_op jit(solution)/shard_map/reduce_scatter | solution.py:64
  83.0 79.2 %reduce-scatter.7.cloned.1.call-start = ((), (), s32[]{:S(2)}) async-start(), calls=%async_computation.8 | async-start | bytes 1433600 | tf_op jit(solution)/shard_map/reduce_scatter | solution.py:64
  91.9 101.0 %all-gather.8.cloned.1.call-start = ((), (), s32[]{:S(2)}) async-start(), calls=%async_computation.10 | async-start | bytes 1433600 | tf_op jit(solution)/shard_map/all_gather | solution.py:71
  164.6 59.3 %all-gather.10.cloned.1.call-start = ((), (), s32[]{:S(2)}) async-start(), calls=%async_computation.11 | async-start | bytes 1433600 | tf_op jit(solution)/shard_map/all_gather | solution.py:71
  165.2 103.7 %reduce-scatter.11.cloned.1.call-start = ((), (), s32[]{:S(2)}) async-start(), calls=%async_computation.12 | async-start | bytes 589824 | tf_op jit(solution)/shard_map/reduce_scatter | solution.py:84
  233.9 2.1 copy-start.1
  235.2 64.9 %all-gather.12.cloned.1.call-start = ((), (), s32[]{:S(2)}) async-start(), calls=%async_computation.13 | async-start | bytes 1433600 | tf_op jit(solution)/shard_map/all_gather | solution.py:71
  236.0 7.6 %copy-start = (bf16[320,1792]{1,0:T(8,128)(2,1)S(1)}, bf16[320,1792]{1,0:T(8,128)(2,1)}, u32[]{:S(2)}) copy-start(bf16[320,1792]{1,0:T(8,128)(2,1)} %all-gather.8.cloned.1.call-done) | copy-start | bytes 3440644
  268.9 40.1 %all-to-all-start.1 = ((bf16[4,8,1024]{2,1,0:T(8,128)(2,1)}), bf16[4,8,1024]{2,1,0:T(8,128)(2,1)S(1)}, u32[]{:S(2)}, u32[]{:S(2)}) async-start(bf16[4,8,1024]{2,1,0:T(8,128)(2,1)} %bitcast.81), calls=%async_computation.5 | async-start | bytes 131072 | tf_op jit(solution)/shard_map/all_to_all | solution.py:87
Sparse Core Ops, SparseCore 0:
  30.0 22.5 all-gather.5
  73.8 27.8 reduce-scatter.4
  104.6 27.3 reduce-scatter.8
  134.8 27.3 reduce-scatter.6
  164.7 28.1 all-gather.7
  194.9 28.9 all-gather.9
  235.4 33.4 reduce-scatter.10
  270.5 29.6 all-gather.11
where the time goes:
time: 317 us; the launch traced here: 316 us
  waiting for transfers between devices  164 us (52%)
  matrix products  74.7 us (24%)
  blocking collectives  42.8 us (14%)
  between operations  14.4 us (5%)
  local copies, waits for them, and re-layouts  10.4 us (3%)
  starting transfers between devices  5.12 us (2%)
  other arithmetic  4.6 us (1%)
    all_gather x3, waiting for transfers between devices, spread(): whole = lax.all_gather(part, 'dp', axis=0, tiled=True)  75.1 us
    reduce_scatter x3, waiting for transfers between devices, summed(): lax.psum_scatter(part, 'dp', scatter_dimension=0, tiled=True).astype(f32)  70.3 us
    all_gather x1, blocking collectives, shards(): route = lax.all_gather(route, ('dp', 'expert'), axis=0, tiled=True)  30.6 us
    dot_general x3, matrix products, summed(): jnp.einsum(spec, left, right, preferred_element_type=f32).astype(bf16)  28.5 us
    reduce_scatter x1, waiting for transfers between devices, shards(): lax.psum_scatter(token_part, ('expert', 'tensor'), scatter_dimension=0, t...  17.7 us
    all_to_all x1, blocking collectives, shards(): both = lax.all_to_all(both, 'dp', split_axis=2, concat_axis=1, tiled=True)  12.2 us
    dot_general x1, matrix products, shards(): jnp.einsum('lnf,ldf->lnd', up_delta, w_up, preferred_element_type=f32)  10 us
    dot_general x1, matrix products, shards(): jnp.einsum('lnf,ldf->lnd', gate_delta, w_gate, preferred_element_type=f32)  10 us
  transfers between devices with their start and end apart: 9, of which 7 were waited for; matrix products, arithmetic and copies ran while one was open for 17% of the time, Pallas kernels for 0%

commit v1 on v0

v1 whole, which is shorter than its diff:
```python
import functools

import jax
import jax.numpy as jnp
from jax import lax
from jax.experimental import pallas as pl
from jax.experimental.pallas import tpu as pltpu
from jax.sharding import PartitionSpec as P

EXPERTS = 8
TOP = 2
F32 = jnp.float32
BF16 = jnp.bfloat16
MESH = pl.DeviceIdType.MESH
NT = (((1,), (1,)), ((), ()))
TN = (((0,), (0,)), ((), ()))


class Sizes:
    def __init__(self, n, e, t, held, width, local, hidden):
        self.n, self.e, self.t, self.held = n, e, t, held
        self.pairs = t // 2
        self.plane = e * self.pairs
        self.groups = n * e
        self.block_rows = held * t
        self.tokens = self.groups * self.block_rows
        self.width = width
        self.slice = width // n
        self.capacity = 5 * self.block_rows * TOP // (4 * EXPERTS)
        self.local = local
        self.rows = self.groups * self.capacity
        self.all_rows = local * self.rows
        self.hidden = hidden
        self.cols = 256 if hidden % 256 == 0 else 128
        self.chunks = hidden // self.cols
        self.unit_rows = self.all_rows // 2
        self.per_unit = local // 2 if local >= 2 else 1
        self.part_rows = self.unit_rows // self.per_unit
        self.units = 2 * self.chunks
        self.down_slots = min(4, self.chunks)


def exchange_kernel(
    s,
    tok, dout, route, wg_hbm, wu_hbm, wd_hbm,
    token_grad, x_out, g_out, res_out,
    xy, routes, xtok, ytok, table, x, g, wg, wu, wd, send, recv_a, recv_b, res, pend, rg, tp, pair_in, sum_a,
    plane_in, sum_b,
    wsem, zs, zr, rs, rr, ps, pr, ds, dr, s1, r1, s2, r2, s3, r3, es, er, fs, fr, hs, hr, osem,
):
    n, W, C, FC = s.n, s.slice, s.chunks, s.cols
    z, e, t = (lax.axis_index(a) for a in ("dp", "expert", "tensor"))
    t2, par = t // 2, t % 2
    spot = e * s.pairs + t2
    group = z * s.e + e

    def remote(src, dst, ssem, rsem, dev):
        return pltpu.make_async_remote_copy(
            src_ref=src, dst_ref=dst, send_sem=ssem, recv_sem=rsem, device_id=dev, device_id_type=MESH
        )

    def plane_dev(q):
        return {"expert": q // s.pairs, "tensor": (q % s.pairs) * 2 + par}

    def group_dev(k):
        return {"dp": k // s.e, "expert": k % s.e}

    other = {"tensor": t2 * 2 + (1 - par)}

    def gate_load(c):
        return pltpu.make_async_copy(
            wg_hbm.at[:, :, pl.ds(c * FC, FC)], wg.at[:, :, pl.ds(c * FC, FC)], wsem.at[0, c])

    def up_load(c):
        return pltpu.make_async_copy(
            wu_hbm.at[:, :, pl.ds(c * FC, FC)], wu.at[:, :, pl.ds(c * FC, FC)], wsem.at[1, c])

    def down_load(c):
        return pltpu.make_async_copy(
            wd_hbm.at[:, pl.ds(c * FC, FC), :], wd.at[lax.rem(c, s.down_slots)], wsem.at[2, c])

    for c in range(C):
        gate_load(c).start()
        up_load(c).start()
        if c < s.down_slots:
            down_load(c).start()

    barrier = pltpu.get_barrier_semaphore()

    def greet(dev):
        pl.semaphore_signal(barrier, inc=1, device_id=dev, device_id_type=MESH)

    def greet_group(k, _):
        greet(group_dev(lax.rem(group + k, s.groups)))
        return 0

    def greet_plane(k, _):
        greet(plane_dev(lax.rem(spot + k, s.plane)))
        return 0

    lax.fori_loop(1, s.groups, greet_group, 0)
    lax.fori_loop(1, s.plane, greet_plane, 0)
    greet(other)
    pl.semaphore_wait(barrier, s.groups - 1 + s.plane - 1 + 1)

    def z_copy(d, i):
        to = lax.rem(z + d, n)
        src = (tok, dout)[i].at[:, pl.ds(pl.multiple_of(to * W, W), W)]
        return remote(src, xy.at[z, e, t2, par, i], zs.at[d, i], zr.at[d, i], {"dp": to})

    def z_arrival(d, i):
        frm = lax.rem(z + n - d, n)
        dst = xy.at[frm, e, t2, par, i]
        return remote(dst, dst, zs.at[d, i], zr.at[d, i], {"dp": lax.rem(z + d, n)})

    for d in range(1, n):
        for i in range(2):
            z_copy(d, i).start()

    def route_copy(k):
        return remote(route, routes.at[k], rs.at[k], rr.at[k], group_dev(lax.rem(group + k, s.groups)))

    def own_copy(k, i):
        src = (tok, dout)[i].at[:, pl.ds(pl.multiple_of(z * W, W), W)]
        return remote(src, xy.at[z, e, t2, par, i], ps.at[0, k, i], pr.at[0, k, i],
                      plane_dev(lax.rem(spot + k, s.plane)))

    def pass_copy(d, k):
        ref = xy.at[lax.rem(z + n - d, n), e, t2, par]
        return remote(ref, ref, ps.at[d, k, 0], pr.at[d, k, 0], plane_dev(lax.rem(spot + k, s.plane)))

    def own_arrival(k, i):
        q = lax.rem(spot + s.plane - k, s.plane)
        ref = xy.at[z, q // s.pairs, lax.rem(q, s.pairs), par, i]
        return remote(ref, ref, ps.at[0, k, i], pr.at[0, k, i], plane_dev(q))

    def pass_arrival(d, k):
        q = lax.rem(spot + s.plane - k, s.plane)
        ref = xy.at[lax.rem(z + n - d, n), q // s.pairs, lax.rem(q, s.pairs), par]
        return remote(ref, ref, ps.at[d, k, 0], pr.at[d, k, 0], plane_dev(q))

    def core_copy(d):
        ref = xy.at[lax.rem(z + n - d, n), :, :, par]
        return remote(ref, ref, ds.at[d], dr.at[d], other)

    def core_arrival(d):
        ref = xy.at[lax.rem(z + n - d, n), :, :, 1 - par]
        return remote(ref, ref, ds.at[d], dr.at[d], other)

    def loop(lo, hi, fn):
        lax.fori_loop(lo, hi, lambda k, c: (fn(k), c)[1], 0)

    def own_send(k):
        own_copy(k, 0).start()
        own_copy(k, 1).start()

    loop(1, s.plane, own_send)
    loop(1, s.groups, lambda k: route_copy(k).start())
    xy[z, e, t2, par, 0] = tok[:, pl.ds(pl.multiple_of(z * W, W), W)]
    xy[z, e, t2, par, 1] = dout[:, pl.ds(pl.multiple_of(z * W, W), W)]
    for d in range(1, n):
        z_arrival(d, 0).wait_recv()
        z_arrival(d, 1).wait_recv()
        loop(1, s.plane, lambda k: pass_copy(d, k).start())

    rg[...] = jnp.zeros_like(rg)

    def own_wait(k):
        own_arrival(k, 0).wait_recv()
        own_arrival(k, 1).wait_recv()

    loop(1, s.plane, own_wait)
    core_copy(0).start()
    for d in range(1, n):
        loop(1, s.plane, lambda k: pass_arrival(d, k).wait_recv())
        core_copy(d).start()
    loop(1, s.groups, lambda k: route_copy(k).wait_recv())
    for d in range(n):
        core_arrival(d).wait_recv()

    def order(i):
        at = (i // s.plane, lax.rem(i, s.plane) // s.pairs, lax.rem(i, s.pairs))
        rows = pl.ds(pl.multiple_of(i * 2 * s.held, 2 * s.held), 2 * s.held)
        for k, ref in enumerate((xtok, ytok)):
            two = [xy[at[0], at[1], at[2], p, k].astype(F32) for p in range(2)]
            ref[rows, :] = jnp.concatenate(two, 0).astype(BF16)

    loop(0, n * s.plane, order)

    total = lax.fori_loop(1, s.groups, lambda k, acc: acc + routes[k], route[...])
    lane = lax.broadcasted_iota(jnp.int32, (1, s.tokens), 1)
    block = (lane // s.block_rows).astype(F32)
    first = (e * s.local).astype(F32)
    targets, probs = [], []
    for k in range(TOP):
        local = total[TOP + k : TOP + k + 1] - first
        slot = total[2 * TOP + k : 2 * TOP + k + 1]
        keep = (slot < s.capacity) & (local >= 0.0) & (local < s.local)
        targets.append(jnp.where(keep, local * s.rows + block * s.capacity + slot, -1.0))
        probs.append(total[k : k + 1])
    step = 80 if s.all_rows % 80 == 0 else 16

    def dispatch(i):
        rows = pl.ds(pl.multiple_of(i * step, step), step)
        place = (lax.broadcasted_iota(jnp.int32, (step, s.tokens), 0) + i * step).astype(F32)
        hit = [place == targets[k] for k in range(TOP)]
        one = jnp.where(hit[0] | hit[1], 1.0, 0.0).astype(BF16)
        table[rows, :] = one
        weight = jnp.where(hit[0], probs[0], 0.0) + jnp.where(hit[1], probs[1], 0.0)
        weight = jnp.sum(weight, axis=1, keepdims=True)
        x[rows, :] = jnp.dot(one, xtok[...], preferred_element_type=F32).astype(BF16)
        g[rows, :] = (weight * jnp.dot(one, ytok[...], preferred_element_type=F32)).astype(BF16)

    loop(0, s.all_rows // step, dispatch)
    x_copy = pltpu.make_async_copy(x, x_out, osem.at[0])
    g_copy = pltpu.make_async_copy(g, g_out, osem.at[1])
    x_copy.start()
    g_copy.start()

    inner = jnp.where(z < n // 2, n // 2 - 1, n // 2)
    is_mid = z == inner
    across = n - 1 - z
    outer = jnp.where(z < n // 2, z - 1, z + 1)

    def unit(u):
        return u // 2, lax.rem(u, 2)

    def part(ref, u):
        c, h = unit(u)
        return ref.at[c, :, pl.ds(pl.multiple_of(h * s.unit_rows, s.unit_rows), s.unit_rows), :]

    def expert_of(h, j):
        return h * s.per_unit + j if s.local >= 2 else 0

    def row_at(h, j):
        return pl.multiple_of(h * s.unit_rows + j * s.part_rows, 16)

    def forward(u, put):
        c, h = unit(u)

        @pl.when(h == 0)
        def _():
            gate_load(c).wait()
            up_load(c).wait()
            down_load(c).wait()

        columns = pl.ds(pl.multiple_of(c * FC, FC), FC)
        for j in range(s.per_unit):
            l = expert_of(h, j)
            rows = pl.ds(row_at(h, j), s.part_rows)
            xs, gs = x[rows, :], g[rows, :]
            put(0, c, h, j, jnp.dot(xs, wg[l, :, columns], preferred_element_type=F32))
            put(1, c, h, j, jnp.dot(xs, wu[l, :, columns], preferred_element_type=F32))
            put(2, c, h, j, lax.dot_general(
                gs, wd[lax.rem(c, s.down_slots), l], NT, preferred_element_type=F32))

        @pl.when((h == 1) & (c + s.down_slots < C))
        def _():
            down_load(c + s.down_slots).start()

    def backward(u):
        c, h = unit(u)
        columns = pl.ds(pl.multiple_of(c * FC, FC), FC)
        for j in range(s.per_unit):
            l = expert_of(h, j)
            rows = pl.ds(row_at(h, j), s.part_rows)
            add = lax.dot_general(res[c, 1, rows, :], wg[l, :, columns], NT, preferred_element_type=F32)
            add = add + lax.dot_general(res[c, 2, rows, :], wu[l, :, columns], NT, preferred_element_type=F32)
            rg[rows, :] += add

    def res_copy(u):
        return pltpu.make_async_copy(part(res, u), part(res_out, u), osem.at[2 + u])

    def to_inner(u):
        return remote(part(send, u), part(recv_a, u), s1.at[u], r1.at[u], {"dp": inner})

    def to_across(u):
        return remote(part(send, u), part(recv_b, u), s2.at[u], r2.at[u], {"dp": across})

    def to_outer(u):
        return remote(part(res, u), part(res, u), s3.at[u], r3.at[u], {"dp": outer})

    @pl.when(jnp.logical_not(is_mid))
    def _():
        def first_half(u):
            def put(i, c, h, j, v):
                send[c, i, pl.ds(row_at(h, j), s.part_rows), :] = v.astype(BF16)

            forward(u, put)
            to_inner(u).start()

        loop(0, s.units, first_half)

        def second_half(u):
            remote(part(res, u), part(res, u), s3.at[u], r3.at[u], {"dp": inner}).wait_recv()
            res_copy(u).start()
            backward(u)

        loop(0, s.units, second_half)
        loop(0, s.units, lambda u: to_inner(u).wait_send())

    @pl.when(is_mid)
    def _():
        tile = 16

        def tiles(fn):
            loop(0, s.unit_rows // tile, lambda i: fn(pl.multiple_of(i * tile, tile)))

        def stage_a(u):
            slot = lax.rem(u, 2)
            c, h = unit(u)

            def put(i, c, h, j, v):
                pend[slot, i, pl.ds(j * s.part_rows, s.part_rows), :] = v

            forward(u, put)
            remote(part(recv_a, u), part(recv_a, u), s1.at[u], r1.at[u], {"dp": outer}).wait_recv()

            def add(r):
                here = pl.ds(r, tile)
                there = pl.ds(pl.multiple_of(h * s.unit_rows + r, tile), tile)
                for i in range(3):
                    v = pend[slot, i, here, :] + recv_a[c, i, there, :].astype(F32)
                    pend[slot, i, here, :] = v
                    send[c, i, there, :] = v.astype(BF16)

            tiles(add)
            to_across(u).start()

        def stage_b(u):
            slot = lax.rem(u, 2)
            c, h = unit(u)
            to_across(u).wait_recv()

            def act(r):
                here = pl.ds(r, tile)
                there = pl.ds(pl.multiple_of(h * s.unit_rows + r, tile), tile)
                pg, pu, gh = (
                    pend[slot, i, here, :] + recv_b[c, i, there, :].astype(F32) for i in range(3)
                )
                sg = jax.nn.sigmoid(pg)
                silu = pg * sg
                res[c, 0, there, :] = (silu * pu).astype(BF16)
                res[c, 1, there, :] = (gh * pu * sg * (1.0 + pg * (1.0 - sg))).astype(BF16)
                res[c, 2, there, :] = (gh * silu).astype(BF16)

            tiles(act)
            to_outer(u).start()
            res_copy(u).start()
            backward(u)

        stage_a(0)

        def both(u):
            stage_a(u)
            stage_b(u - 1)

        loop(1, s.units, both)
        stage_b(s.units - 1)
        loop(0, s.units, lambda u: to_across(u).wait_send())
        loop(0, s.units, lambda u: to_outer(u).wait_send())

    span = 128 if s.tokens % 128 == 0 else s.tokens
    per = span // (2 * s.held)
    rows16 = rg[...].astype(BF16)

    def combine(i):
        lanes = pl.ds(pl.multiple_of(i * span, span), span)
        out = lax.dot_general(table[:, lanes], rows16, TN, preferred_element_type=F32)
        for j in range(per):
            k = i * per + j
            at = (k // s.plane, lax.rem(k, s.plane) // s.pairs, lax.rem(k, s.pairs))
            for p in range(2):
                lo = (2 * j + p) * s.held
                tp[at[0], at[1], at[2], p] = out[lo : lo + s.held].astype(BF16)

    loop(0, s.tokens // span, combine)
    pair_copy = remote(tp.at[:, :, :, 1 - par], pair_in, es, er, other)
    pair_copy.start()
    pair_copy.wait_recv()

    def pair_sum(i):
        at = (i // s.plane, lax.rem(i, s.plane) // s.pairs, lax.rem(i, s.pairs))
        v = tp[at[0], at[1], at[2], par].astype(F32) + pair_in[at].astype(F32)
        sum_a[at] = v.astype(BF16)

    loop(0, n * s.plane, pair_sum)

    def plane_copy(k):
        q = lax.rem(spot + k, s.plane)
        return remote(sum_a.at[:, q // s.pairs, lax.rem(q, s.pairs)], plane_in.at[k], fs.at[k], fr.at[k],
                      plane_dev(q))

    loop(1, s.plane, lambda k: plane_copy(k).start())
    loop(1, s.plane, lambda k: plane_copy(k).wait_recv())

    def last(d):
        to = lax.rem(z + d, n)
        v = sum_a[to, e, t2].astype(F32)
        return to, lax.fori_loop(1, s.plane, lambda k, a: a + plane_in[k, to].astype(F32), v).astype(BF16)

    def final_copy(d):
        to = lax.rem(z + d, n)
        return remote(sum_b.at[to], token_grad.at[:, pl.ds(pl.multiple_of(z * W, W), W)], hs.at[d], hr.at[d],
                      {"dp": to})

    def final_arrival(d):
        frm = lax.rem(z + n - d, n)
        return remote(sum_b.at[frm], token_grad.at[:, pl.ds(pl.multiple_of(frm * W, W), W)], hs.at[d], hr.at[d],
                      {"dp": frm})

    for d in range(1, n):
        to, v = last(d)
        sum_b[to] = v
        final_copy(d).start()
    _, v = last(0)
    token_grad[:, pl.ds(pl.multiple_of(z * W, W), W)] = v

    for d in range(1, n):
        for i in range(2):
            z_copy(d, i).wait_send()
        loop(1, s.plane, lambda k: pass_copy(d, k).wait_send())
        core_copy(d).wait_send()

    def own_sent(k):
        own_copy(k, 0).wait_send()
        own_copy(k, 1).wait_send()

    loop(1, s.plane, own_sent)
    core_copy(0).wait_send()
    loop(1, s.groups, lambda k: route_copy(k).wait_send())
    pair_copy.wait_send()
    loop(1, s.plane, lambda k: plane_copy(k).wait_send())
    x_copy.wait()
    g_copy.wait()
    loop(0, s.units, lambda u: res_copy(u).wait())
    for d in range(1, n):
        final_copy(d).wait_send()
        final_arrival(d).wait_recv()


def exchange(s, tokens, out_grad, route, w_gate, w_up, w_down):
    n, E, T2, M, held, W = s.n, s.e, s.pairs, s.plane, s.held, s.slice
    R, C, FC, L, U = s.all_rows, s.chunks, s.cols, s.local, s.units
    vmem = pl.BlockSpec(memory_space=pltpu.VMEM)
    anywhere = pl.BlockSpec(memory_space=pl.ANY)
    dma = pltpu.SemaphoreType.DMA
    return pl.pallas_call(
        functools.partial(exchange_kernel, s),
        out_shape=(
            jax.ShapeDtypeStruct((held, s.width), BF16),
            jax.ShapeDtypeStruct((R, W), BF16),
            jax.ShapeDtypeStruct((R, W), BF16),
            jax.ShapeDtypeStruct((C, 3, R, FC), BF16),
        ),
        in_specs=[vmem] * 3 + [anywhere] * 3,
        out_specs=(vmem, anywhere, anywhere, anywhere),
        scratch_shapes=[
            pltpu.VMEM((n, E, T2, 2, 2, held, W), BF16),
            pltpu.VMEM((s.groups, 8, s.tokens), F32),
            pltpu.VMEM((s.tokens, W), BF16),
            pltpu.VMEM((s.tokens, W), BF16),
            pltpu.VMEM((R, s.tokens), BF16),
            pltpu.VMEM((R, W), BF16),
            pltpu.VMEM((R, W), BF16),
            pltpu.VMEM((L, W, s.hidden), BF16),
            pltpu.VMEM((L, W, s.hidden), BF16),
            pltpu.VMEM((s.down_slots, L, FC, W), BF16),
            pltpu.VMEM((C, 3, R, FC), BF16),
            pltpu.VMEM((C, 3, R, FC), BF16),
            pltpu.VMEM((C, 3, R, FC), BF16),
            pltpu.VMEM((C, 3, R, FC), BF16),
            pltpu.VMEM((2, 3, s.unit_rows, FC), F32),
            pltpu.VMEM((R, W), F32),
            pltpu.VMEM((n, E, T2, 2, held, W), BF16),
            pltpu.VMEM((n, E, T2, held, W), BF16),
            pltpu.VMEM((n, E, T2, held, W), BF16),
            pltpu.VMEM((M, n, held, W), BF16),
            pltpu.VMEM((n, held, W), BF16),
            dma((3, C)),
            dma((n, 2)), dma((n, 2)),
            dma((s.groups,)), dma((s.groups,)),
            dma((n, M, 2)), dma((n, M, 2)),
            dma((n,)), dma((n,)),
            dma((U,)), dma((U,)), dma((U,)), dma((U,)), dma((U,)), dma((U,)),
            dma, dma,
            dma((M,)), dma((M,)),
            dma((n,)), dma((n,)),
            dma((2 + U,)),
        ],
        compiler_params=pltpu.CompilerParams(
            collective_id=0, has_side_effects=True, vmem_limit_bytes=67_043_328),
        name="exchange",
    )(tokens, out_grad, route, w_gate, w_up, w_down)


def grads_kernel(s, many, x, g, res, gate, up, down):
    for j in range(many):
        rows = pl.ds(j * s.rows, s.rows)
        at = pl.ds(pl.multiple_of((pl.program_id(1) * many + j) * s.rows, 16), s.rows)
        xs, gs = x[at, :], g[at, :]
        gate[j] = lax.dot_general(xs, res[0, 1, rows, :], TN, preferred_element_type=F32).astype(BF16)
        up[j] = lax.dot_general(xs, res[0, 2, rows, :], TN, preferred_element_type=F32).astype(BF16)
        down[j] = lax.dot_general(res[0, 0, rows, :], gs, TN, preferred_element_type=F32).astype(BF16)


def weight_grads(s, x, g, res):
    many = 2 if s.local % 2 == 0 else 1
    W, R, FC = s.slice, s.all_rows, s.cols
    whole = pl.BlockSpec(memory_space=pltpu.VMEM)
    wide = pl.BlockSpec((many, W, FC), lambda c, l: (l, 0, c))
    tall = pl.BlockSpec((many, FC, W), lambda c, l: (l, c, 0))
    return pl.pallas_call(
        functools.partial(grads_kernel, s, many),
        grid=(s.chunks, s.local // many),
        out_shape=(
            jax.ShapeDtypeStruct((s.local, W, s.hidden), BF16),
            jax.ShapeDtypeStruct((s.local, W, s.hidden), BF16),
            jax.ShapeDtypeStruct((s.local, s.hidden, W), BF16),
        ),
        in_specs=[whole, whole, pl.BlockSpec((1, 3, many * s.rows, FC), lambda c, l: (c, 0, l, 0))],
        out_specs=(wide, wide, tall),
        compiler_params=pltpu.CompilerParams(dimension_semantics=("arbitrary", "arbitrary")),
        name="weight_grads",
    )(x, g, res)


def shards(tokens, out_grad, route_probs, expert_ids, slot_index, w_gate, w_up, w_down):
    n, e, t = (lax.axis_size(a) for a in ("dp", "expert", "tensor"))
    held, width = tokens.shape
    s = Sizes(n, e, t, held, width, w_gate.shape[0], w_gate.shape[2])
    own = lax.axis_index("dp") * e + lax.axis_index("expert")
    rows = [route_probs, expert_ids.astype(F32), slot_index.astype(F32)]
    rows = jnp.concatenate(rows + [jnp.zeros((s.block_rows, 8 - 3 * TOP), F32)], axis=1).T
    here = lax.broadcasted_iota(jnp.int32, (8, s.groups, s.block_rows), 1) == own
    route = jnp.where(here, rows[:, None, :], 0.0).reshape(8, s.tokens)
    token_grad, x, g, res = exchange(s, tokens, out_grad, route, w_gate, w_up, w_down)
    gate, up, down = weight_grads(s, x, g, res)
    return token_grad, gate, up, down


def solution(mesh):
    placed = (
        P(("dp", "expert", "tensor"), None),
        P(("dp", "expert", "tensor"), None),
        P(("dp", "expert"), None),
        P(("dp", "expert"), None),
        P(("dp", "expert"), None),
        P("expert", "dp", "tensor"),
        P("expert", "dp", "tensor"),
        P("expert", "tensor", "dp"),
    )
    return jax.shard_map(
        shards,
        mesh=mesh,
        in_specs=placed,
        out_specs=(
            P(("dp", "expert", "tensor"), None),
            P("expert", "dp", "tensor"),
            P("expert", "dp", "tensor"),
            P("expert", "tensor", "dp"),
        ),
        check_vma=False,
    )
```

time: 317 us -> 149 us (0.47)
  waiting for transfers between devices: 164 us -> 0 us
  Pallas kernels: 0 us -> 143 us
  matrix products: 74.7 us -> 0 us
  blocking collectives: 42.8 us -> 0 us
  between operations: 14.4 us -> 0.66 us
  local copies, waits for them, and re-layouts: 10.4 us -> 1.8 us
  starting transfers between devices: 5.12 us -> 0 us
    pallas_call x0 -> x2, Pallas kernels: none -> 143 us  [the longest x1 123 us: exchange(): pl.pallas_call(functools.partial(exchange_kernel, s), out_shape=(jax.Shap...]
    reduce_scatter x4 -> x0, waiting for transfers between devices: 88 us -> none  [the longest x3 70.3 us: summed(): lax.psum_scatter(part, 'dp', scatter_dimension=0, tiled=True).astype(f32)]
    all_gather x4 -> x0, waiting for transfers between devices: 75.1 us -> none  [the longest x3 75.1 us: spread(): whole = lax.all_gather(part, 'dp', axis=0, tiled=True)]
    dot_general x11 -> x0, matrix products: 74.7 us -> none  [the longest x3 28.5 us: summed(): jnp.einsum(spec, left, right, preferred_element_type=f32).astype(bf16)]
    all_gather x1 -> x0, blocking collectives: 30.6 us -> none  [shards(): route = lax.all_gather(route, ('dp', 'expert'), axis=0, tiled=True)]
    all_to_all x1 -> x0, blocking collectives: 12.2 us -> none  [shards(): both = lax.all_to_all(both, 'dp', split_axis=2, concat_axis=1, tiled=True)]
    all_to_all x1 -> x0, starting transfers between devices: 4.61 us -> none  [shards(): lax.all_to_all(token_part, 'dp', split_axis=0, concat_axis=1, tiled=True)]
    unnamed x15 -> x1, local copies, waits for them, and re-layouts: 5.29 us -> 1.47 us
  transfers between devices with their start and end apart: 9 -> 0, of which waited for: 7 -> 0; matrix products, arithmetic and copies ran while one was open for 17% -> 0% of each run, Pallas kernels for 0% -> 0%
where the time goes in v1:
time: 149 us; the launch traced here: 148 us
  Pallas kernels  143 us (96%)
  other arithmetic  2.72 us (2%)
  local copies, waits for them, and re-layouts  1.8 us (1%)
    pallas_call x1, Pallas kernels, exchange(): pl.pallas_call(functools.partial(exchange_kernel, s), out_shape=(jax.Shap...  123 us
    pallas_call x1, Pallas kernels, weight_grads(): pl.pallas_call(functools.partial(grads_kernel, s, many), grid=(s.chunks,...  20 us

profile of v1, /device:TPU:0, one launch (start us, length us, event | category | flops | bytes accessed | tf_op | source)
XLA Modules:
  0.0 148.3 jit_solution(5201833717105105606)
XLA Ops:
  0.6 0.1 iota.11
  0.7 0.1 iota.12
  0.8 0.1 pad.3.clone
  0.9 0.7 convert_element_type.6
  1.6 0.7 convert_element_type.7
  2.3 0.7 maximum_bitcast_fusion
  3.0 0.1 broadcast_in_dim.20
  3.1 0.6 broadcast_select_fusion.route
  3.7 123.1 %exchange.1 = (bf16[8,4096]{1,0:T(8,128)(2,1)}, bf16[320,1024]{1,0:T(8,128)(2,1)}, bf16[320,1024]{1,0:T(8,128)(2,1)}, bf16[7,3,320,256]{3,2,1,0:T(8,128)(2,1)}) custom-call(bf16[8,4096]{1,0:T(8,128)(2,1)} %tok.1, bf16[8,4096]{1,0:T(8,128)(2,1)} %dout.1, f32[8,256]{1,0:T(8,128)} %broadcast_select_fusion.route, bf16[4,1024,1792]{2,1,0:T(8,128)(2,1)} %wg_hbm.1, ...), custom_call_target="tpu_custom_call" | custom-call | tf_op jit(solution)/shard_map/exchange/pallas_call | solution.py:448
  126.8 20.0 %weight_grads.1 = (bf16[4,1024,1792]{2,1,0:T(8,128)(2,1)}, bf16[4,1024,1792]{2,1,0:T(8,128)(2,1)}, bf16[4,1792,1024]{2,1,0:T(8,128)(2,1)}) custom-call(bf16[320,1024]{1,0:T(8,128)(2,1)} %get-tuple-element.12.x, bf16[320,1024]{1,0:T(8,128)(2,1)} %get-tuple-element.13.g, bf16[7,3,320,256]{3,2,1,0:T(8,128)(2,1)} %get-tuple-element.14.res), custom_call_target="tpu_custom_call" | custom-call | tf_op jit(solution)/shard_map/weight_grads/pallas_call | solution.py:513
  146.8 1.5 copy.13
  (3 shorter events, 0.0 us)

commit v2 on v1

v2 whole, which is shorter than its diff:
```python
import functools

import jax
import jax.numpy as jnp
from jax import lax
from jax.experimental import pallas as pl
from jax.experimental.pallas import tpu as pltpu
from jax.sharding import PartitionSpec as P

EXPERTS = 8
TOP = 2
F32 = jnp.float32
BF16 = jnp.bfloat16
MESH = pl.DeviceIdType.MESH
NT = (((1,), (1,)), ((), ()))
TN = (((0,), (0,)), ((), ()))


class Sizes:
    def __init__(self, n, e, t, held, width, local, hidden):
        self.n, self.e, self.t, self.held = n, e, t, held
        self.pairs = t // 2
        self.plane = e * self.pairs
        self.groups = n * e
        self.block_rows = held * t
        self.tokens = self.groups * self.block_rows
        self.width = width
        self.slice = width // n
        self.capacity = 5 * self.block_rows * TOP // (4 * EXPERTS)
        self.local = local
        self.rows = self.groups * self.capacity
        self.all_rows = local * self.rows
        self.hidden = hidden
        self.cols = 256 if hidden % 256 == 0 else 128
        self.chunks = hidden // self.cols
        self.cuts = 4
        self.unit_rows = self.all_rows // self.cuts
        self.per_unit = max(local // self.cuts, 1)
        self.part_rows = self.unit_rows // self.per_unit
        self.units = self.cuts * self.chunks
        self.subs = self.cols // 128
        self.down_slots = min(4, self.chunks)


def exchange_kernel(
    s,
    tok_hbm, dout_hbm, probs_hbm, ids_hbm, slots_hbm, wg_hbm, wu_hbm, wd_hbm,
    token_grad, x_out, g_out, res_out,
    tok, dout, route_probs, expert_ids, slot_index, xy, route, routes, xtok, ytok, table, x, g, wg, wu, wd, send, recv_a, recv_b, res, pend, rg, tp, pair_in, sum_a,
    plane_in, sum_b,
    wsem, zs, zr, rs, rr, ps, pr, ds, dr, s1, r1, r2, s3, es, er, fs, fr, hs, hr, osem, rsem, isem,
):
    n, W, C, FC = s.n, s.slice, s.chunks, s.cols
    z, e, t = (lax.axis_index(a) for a in ("dp", "expert", "tensor"))
    t2, par = t // 2, t % 2
    spot = e * s.pairs + t2
    group = z * s.e + e

    def remote(src, dst, ssem, rsem, dev):
        return pltpu.make_async_remote_copy(
            src_ref=src, dst_ref=dst, send_sem=ssem, recv_sem=rsem, device_id=dev, device_id_type=MESH
        )

    def plane_dev(q):
        return {"expert": q // s.pairs, "tensor": (q % s.pairs) * 2 + par}

    def group_dev(k):
        return {"dp": k // s.e, "expert": k % s.e}

    other = {"tensor": t2 * 2 + (1 - par)}

    barrier = pltpu.get_barrier_semaphore()

    def greet(dev):
        pl.semaphore_signal(barrier, inc=1, device_id=dev, device_id_type=MESH)

    def greet_group(k, _):
        greet(group_dev(lax.rem(group + k, s.groups)))
        return 0

    def greet_plane(k, _):
        greet(plane_dev(lax.rem(spot + k, s.plane)))
        return 0

    lax.fori_loop(1, s.groups, greet_group, 0)
    lax.fori_loop(1, s.plane, greet_plane, 0)
    greet(other)

    small = ((probs_hbm, route_probs), (ids_hbm, expert_ids), (slots_hbm, slot_index), (tok_hbm, tok), (dout_hbm, dout))
    inputs = [pltpu.make_async_copy(a, b, isem.at[i]) for i, (a, b) in enumerate(small)]
    for copy in inputs:
        copy.start()

    def gate_load(c):
        return pltpu.make_async_copy(
            wg_hbm.at[:, :, pl.ds(c * FC, FC)], wg.at[:, :, pl.ds(c * FC, FC)], wsem.at[c])

    def up_load(c):
        return pltpu.make_async_copy(
            wu_hbm.at[:, :, pl.ds(c * FC, FC)], wu.at[:, :, pl.ds(c * FC, FC)], wsem.at[c])

    def down_load(c):
        return pltpu.make_async_copy(
            wd_hbm.at[:, pl.ds(c * FC, FC), :], wd.at[lax.rem(c, s.down_slots)], wsem.at[c])

    for copy in inputs:
        copy.wait()
    for c in range(C):
        gate_load(c).start()
        up_load(c).start()
        if c < s.down_slots:
            down_load(c).start()

    lane = lax.broadcasted_iota(jnp.int32, (TOP, s.tokens), 1)
    mine = lane // s.block_rows == group
    for i, ref in enumerate((route_probs, expert_ids, slot_index)):
        wide = jnp.concatenate([ref[...].astype(F32)] * s.groups, axis=1)
        route[i * TOP : (i + 1) * TOP, :] = jnp.where(mine, wide, 0.0)
    route[3 * TOP :, :] = jnp.zeros((8 - 3 * TOP, s.tokens), F32)

    pl.semaphore_wait(barrier, s.groups - 1 + s.plane - 1 + 1)

    def z_copy(d, i):
        to = lax.rem(z + d, n)
        src = (tok, dout)[i].at[:, pl.ds(pl.multiple_of(to * W, W), W)]
        return remote(src, xy.at[z, e, t2, par, i], zs.at[d], zr.at[d], {"dp": to})

    def z_arrival(d):
        frm = lax.rem(z + n - d, n)
        dst = xy.at[frm, e, t2, par]
        return remote(dst, dst, zs.at[d], zr.at[d], {"dp": lax.rem(z + d, n)})

    for d in range(1, n):
        for i in range(2):
            z_copy(d, i).start()

    def route_copy(k):
        return remote(route, routes.at[k], rs, rr, group_dev(lax.rem(group + k, s.groups)))

    def all_routes():
        ref = routes.at[pl.ds(1, s.groups - 1)]
        return remote(ref, ref, rs, rr, group_dev(lax.rem(group + 1, s.groups)))

    def all_plane(d):
        ref = plane_in.at[pl.ds(1, s.plane - 1), pl.ds(0, 2)]
        return remote(ref, ref, ps.at[d], pr.at[d], plane_dev(lax.rem(spot + 1, s.plane)))

    def own_copy(k, i):
        src = (tok, dout)[i].at[:, pl.ds(pl.multiple_of(z * W, W), W)]
        return remote(src, xy.at[z, e, t2, par, i], ps.at[0], pr.at[0],
                      plane_dev(lax.rem(spot + k, s.plane)))

    def pass_copy(d, k):
        ref = xy.at[lax.rem(z + n - d, n), e, t2, par]
        return remote(ref, ref, ps.at[d], pr.at[d], plane_dev(lax.rem(spot + k, s.plane)))

    def core_copy(d):
        ref = xy.at[lax.rem(z + n - d, n), :, :, par]
        return remote(ref, ref, ds.at[d], dr.at[d], other)

    def core_arrival(d):
        ref = xy.at[lax.rem(z + n - d, n), :, :, 1 - par]
        return remote(ref, ref, ds.at[d], dr.at[d], other)

    def loop(lo, hi, fn):
        lax.fori_loop(lo, hi, lambda k, c: (fn(k), c)[1], 0)

    def own_send(k):
        own_copy(k, 0).start()
        own_copy(k, 1).start()

    loop(1, s.plane, own_send)
    loop(1, s.groups, lambda k: route_copy(k).start())
    xy[z, e, t2, par, 0] = tok[:, pl.ds(pl.multiple_of(z * W, W), W)]
    xy[z, e, t2, par, 1] = dout[:, pl.ds(pl.multiple_of(z * W, W), W)]
    for d in range(1, n):
        z_arrival(d).wait_recv()
        loop(1, s.plane, lambda k: pass_copy(d, k).start())

    rg[...] = jnp.zeros_like(rg)

    for d in range(n):
        all_plane(d).wait_recv()
        core_copy(d).start()
    all_routes().wait_recv()
    for d in range(n):
        core_arrival(d).wait_recv()

    def order(i):
        at = (i // s.plane, lax.rem(i, s.plane) // s.pairs, lax.rem(i, s.pairs))
        rows = pl.ds(pl.multiple_of(i * 2 * s.held, 2 * s.held), 2 * s.held)
        for k, ref in enumerate((xtok, ytok)):
            two = [xy[at[0], at[1], at[2], p, k].astype(F32) for p in range(2)]
            ref[rows, :] = jnp.concatenate(two, 0).astype(BF16)

    loop(0, n * s.plane, order)

    total = lax.fori_loop(1, s.groups, lambda k, acc: acc + routes[k], route[...])
    block = (lax.broadcasted_iota(jnp.int32, (1, s.tokens), 1) // s.block_rows).astype(F32)
    first = (e * s.local).astype(F32)
    targets, probs = [], []
    for k in range(TOP):
        local = total[TOP + k : TOP + k + 1] - first
        slot = total[2 * TOP + k : 2 * TOP + k + 1]
        keep = (slot < s.capacity) & (local >= 0.0) & (local < s.local)
        targets.append(jnp.where(keep, local * s.rows + block * s.capacity + slot, -1.0))
        probs.append(total[k : k + 1])
    step = 80 if s.all_rows % 80 == 0 else 16

    def dispatch(i):
        rows = pl.ds(pl.multiple_of(i * step, step), step)
        place = (lax.broadcasted_iota(jnp.int32, (step, s.tokens), 0) + i * step).astype(F32)
        hit = [place == targets[k] for k in range(TOP)]
        one = jnp.where(hit[0] | hit[1], 1.0, 0.0).astype(BF16)
        table[rows, :] = one
        weight = jnp.where(hit[0], probs[0], 0.0) + jnp.where(hit[1], probs[1], 0.0)
        weight = jnp.sum(weight, axis=1, keepdims=True)
        x[rows, :] = jnp.dot(one, xtok[...], preferred_element_type=F32).astype(BF16)
        g[rows, :] = (weight * jnp.dot(one, ytok[...], preferred_element_type=F32)).astype(BF16)

    loop(0, s.all_rows // step, dispatch)
    x_copy = pltpu.make_async_copy(x, x_out, osem.at[0])
    g_copy = pltpu.make_async_copy(g, g_out, osem.at[1])
    x_copy.start()
    g_copy.start()

    inner = jnp.where(z < n // 2, n // 2 - 1, n // 2)
    is_mid = z == inner
    across = n - 1 - z
    outer = jnp.where(z < n // 2, z - 1, z + 1)

    def unit(u):
        return u // s.cuts, lax.rem(u, s.cuts)

    def part(ref, u):
        c, h = unit(u)
        return ref.at[c, :, pl.ds(pl.multiple_of(h * s.unit_rows, s.unit_rows), s.unit_rows), :]

    def piece(ref, u, b):
        c, h = unit(u)
        rows = pl.ds(pl.multiple_of(h * s.unit_rows, s.unit_rows), s.unit_rows)
        return ref.at[c, :, rows, pl.ds(b * 128, 128)]

    def expert_of(h, j):
        return h * s.per_unit + j if s.local >= s.cuts else h * s.local // s.cuts

    def row_at(h, j):
        return pl.multiple_of(h * s.unit_rows + j * s.part_rows, 16)

    def forward(u, put):
        c, h = unit(u)

        @pl.when(h == 0)
        def _():
            three = wg.at[:, :, pl.ds(0, 3 * FC)]
            pltpu.make_async_copy(three, three, wsem.at[c]).wait()

        columns = pl.ds(pl.multiple_of(c * FC, FC), FC)
        for j in range(s.per_unit):
            l = expert_of(h, j)
            rows = pl.ds(row_at(h, j), s.part_rows)
            xs, gs = x[rows, :], g[rows, :]
            put(0, c, h, j, jnp.dot(xs, wg[l, :, columns], preferred_element_type=F32))
            put(1, c, h, j, jnp.dot(xs, wu[l, :, columns], preferred_element_type=F32))
            put(2, c, h, j, lax.dot_general(
                gs, wd[lax.rem(c, s.down_slots), l], NT, preferred_element_type=F32))

        @pl.when((h == s.cuts - 1) & (c + s.down_slots < C))
        def _():
            down_load(c + s.down_slots).start()

    def backward(u):
        c, h = unit(u)
        columns = pl.ds(pl.multiple_of(c * FC, FC), FC)
        for j in range(s.per_unit):
            l = expert_of(h, j)
            rows = pl.ds(row_at(h, j), s.part_rows)
            add = lax.dot_general(res[c, 1, rows, :], wg[l, :, columns], NT, preferred_element_type=F32)
            add = add + lax.dot_general(res[c, 2, rows, :], wu[l, :, columns], NT, preferred_element_type=F32)
            rg[rows, :] += add

    def res_copy(u):
        return pltpu.make_async_copy(part(res, u), part(res_out, u), rsem)

    def to_inner(u, b):
        return remote(piece(send, u, b), piece(recv_a, u, b), s1, r1.at[u * s.subs + b], {"dp": inner})

    def from_outer(u, b):
        return remote(piece(recv_a, u, b), piece(recv_a, u, b), s1, r1.at[u * s.subs + b], {"dp": outer})

    def to_across(u, b):
        return remote(piece(send, u, b), piece(recv_b, u, b), s1, r2.at[u * s.subs + b], {"dp": across})

    def to_outer(u, b):
        return remote(piece(res, u, b), piece(res, u, b), s3, r1.at[u * s.subs + b], {"dp": outer})

    def from_inner(u, b):
        return remote(piece(res, u, b), piece(res, u, b), s3, r1.at[u * s.subs + b], {"dp": inner})

    @pl.when(jnp.logical_not(is_mid))
    def _():
        def first_half(u):
            def put(i, c, h, j, v):
                send[c, i, pl.ds(row_at(h, j), s.part_rows), :] = v.astype(BF16)

            forward(u, put)
            for b in range(s.subs):
                to_inner(u, b).start()

        loop(0, s.units, first_half)

        def second_half(u):
            for b in range(s.subs):
                from_inner(u, b).wait_recv()
            res_copy(u).start()
            backward(u)

        loop(0, s.units, second_half)
        remote(send, send, s1, r1.at[0], {"dp": inner}).wait_send()

    @pl.when(is_mid)
    def _():
        tile = 16

        def tiles(fn):
            for i in range(s.unit_rows // tile):
                fn(i * tile)

        def ahead(u):
            def put(i, c, h, j, v):
                pend[lax.rem(u, 3), i, pl.ds(j * s.part_rows, s.part_rows), :] = v

            forward(u, put)

        def stage_a(u):
            slot = lax.rem(u, 3)
            c, h = unit(u)

            for b in range(s.subs):
                from_outer(u, b).wait_recv()
                columns = pl.ds(b * 128, 128)

                def add(r):
                    here = pl.ds(r, tile)
                    there = pl.ds(pl.multiple_of(h * s.unit_rows + r, tile), tile)
                    for i in range(3):
                        v = pend[slot, i, here, columns] + recv_a[c, i, there, columns].astype(F32)
                        pend[slot, i, here, columns] = v
                        send[c, i, there, columns] = v.astype(BF16)

                tiles(add)
                to_across(u, b).start()

        def stage_b(u):
            slot = lax.rem(u, 3)
            c, h = unit(u)
            for b in range(s.subs):
                to_across(u, b).wait_recv()
                columns = pl.ds(b * 128, 128)

                def act(r):
                    here = pl.ds(r, tile)
                    there = pl.ds(pl.multiple_of(h * s.unit_rows + r, tile), tile)
                    pg, pu, gh = (
                        pend[slot, i, here, columns] + recv_b[c, i, there, columns].astype(F32) for i in range(3)
                    )
                    sg = jax.nn.sigmoid(pg)
                    silu = pg * sg
                    res[c, 0, there, columns] = (silu * pu).astype(BF16)
                    res[c, 1, there, columns] = (gh * pu * sg * (1.0 + pg * (1.0 - sg))).astype(BF16)
                    res[c, 2, there, columns] = (gh * silu).astype(BF16)

                tiles(act)
                to_outer(u, b).start()
            res_copy(u).start()
            backward(u)

        ahead(0)

        def both(u):
            @pl.when(u < s.units)
            def _():
                stage_a(u)

            @pl.when(u + 1 < s.units)
            def _():
                ahead(u + 1)

            @pl.when(u >= 1)
            def _():
                stage_b(u - 1)

        loop(0, s.units + 1, both)
        remote(send, send, s1, r1.at[0], {"dp": across}).wait_send()
        remote(res, res, s3, r1.at[0], {"dp": outer}).wait_send()

    span = 128 if s.tokens % 128 == 0 else s.tokens
    per = span // (2 * s.held)
    rows16 = rg[...].astype(BF16)

    def combine(i):
        lanes = pl.ds(pl.multiple_of(i * span, span), span)
        out = lax.dot_general(table[:, lanes], rows16, TN, preferred_element_type=F32)
        for j in range(per):
            k = i * per + j
            at = (k // s.plane, lax.rem(k, s.plane) // s.pairs, lax.rem(k, s.pairs))
            for p in range(2):
                lo = (2 * j + p) * s.held
                tp[at[0], at[1], at[2], p] = out[lo : lo + s.held].astype(BF16)

    loop(0, s.tokens // span, combine)
    pair_copy = remote(tp.at[:, :, :, 1 - par], pair_in, es, er, other)
    pair_copy.start()
    pair_copy.wait_recv()

    def pair_sum(i):
        at = (i // s.plane, lax.rem(i, s.plane) // s.pairs, lax.rem(i, s.pairs))
        v = tp[at[0], at[1], at[2], par].astype(F32) + pair_in[at].astype(F32)
        sum_a[at] = v.astype(BF16)

    loop(0, n * s.plane, pair_sum)

    def plane_copy(d, k):
        q, to = lax.rem(spot + k, s.plane), lax.rem(z + d, n)
        return remote(sum_a.at[to, q // s.pairs, lax.rem(q, s.pairs)], plane_in.at[k, to], fs, fr.at[d],
                      plane_dev(q))

    ranks = [n // 2] + [d for d in range(1, n) if d != n // 2] + [0]
    for d in ranks:
        loop(1, s.plane, lambda k: plane_copy(d, k).start())
    all_in = plane_in.at[pl.ds(1, s.plane - 1)]
    sums = remote(all_in, all_in, fs, fr.at[0], plane_dev(lax.rem(spot + 1, s.plane)))

    def last(d):
        to = lax.rem(z + d, n)
        one_in = plane_in.at[pl.ds(1, s.plane - 1), to]
        remote(one_in, one_in, fs, fr.at[d], plane_dev(lax.rem(spot + 1, s.plane))).wait_recv()
        v = sum_a[to, e, t2].astype(F32)
        return to, lax.fori_loop(1, s.plane, lambda k, a: a + plane_in[k, to].astype(F32), v).astype(BF16)

    def final_copy(d):
        to = lax.rem(z + d, n)
        return remote(sum_b.at[to], token_grad.at[:, pl.ds(pl.multiple_of(z * W, W), W)], hs.at[d], hr.at[d],
                      {"dp": to})

    def final_arrival(d):
        frm = lax.rem(z + n - d, n)
        return remote(sum_b.at[frm], token_grad.at[:, pl.ds(pl.multiple_of(frm * W, W), W)], hs.at[d], hr.at[d],
                      {"dp": frm})

    for d in ranks[:-1]:
        to, v = last(d)
        sum_b[to] = v
        final_copy(d).start()
    _, v = last(0)
    sum_b[z] = v
    own_out = pltpu.make_async_copy(
        sum_b.at[z], token_grad.at[:, pl.ds(pl.multiple_of(z * W, W), W)], osem.at[2])
    own_out.start()

    for d in range(n):
        if d > 0:
            z_arrival(d).wait_send()
        all_plane(d).wait_send()
        core_copy(d).wait_send()
    all_routes().wait_send()
    pair_copy.wait_send()
    sums.wait_send()
    x_copy.wait()
    g_copy.wait()
    own_out.wait()
    pltpu.make_async_copy(res, res_out, rsem).wait()
    for d in range(1, n):
        final_copy(d).wait_send()
        final_arrival(d).wait_recv()


def exchange(s, *args):
    n, E, T2, M, held, W = s.n, s.e, s.pairs, s.plane, s.held, s.slice
    R, C, FC, L, U = s.all_rows, s.chunks, s.cols, s.local, s.units
    anywhere = pl.BlockSpec(memory_space=pl.ANY)
    dma = pltpu.SemaphoreType.DMA
    return pl.pallas_call(
        functools.partial(exchange_kernel, s),
        out_shape=(
            jax.ShapeDtypeStruct((held, s.width), BF16),
            jax.ShapeDtypeStruct((R, W), BF16),
            jax.ShapeDtypeStruct((R, W), BF16),
            jax.ShapeDtypeStruct((C, 3, R, FC), BF16),
        ),
        in_specs=[anywhere] * 8,
        out_specs=(anywhere,) * 4,
        scratch_shapes=[
            pltpu.VMEM((held, s.width), BF16),
            pltpu.VMEM((held, s.width), BF16),
            pltpu.VMEM((TOP, s.block_rows), F32),
            pltpu.VMEM((TOP, s.block_rows), jnp.int32),
            pltpu.VMEM((TOP, s.block_rows), jnp.int32),
            pltpu.VMEM((n, E, T2, 2, 2, held, W), BF16),
            pltpu.VMEM((8, s.tokens), F32),
            pltpu.VMEM((s.groups, 8, s.tokens), F32),
            pltpu.VMEM((s.tokens, W), BF16),
            pltpu.VMEM((s.tokens, W), BF16),
            pltpu.VMEM((R, s.tokens), BF16),
            pltpu.VMEM((R, W), BF16),
            pltpu.VMEM((R, W), BF16),
            pltpu.VMEM((L, W, s.hidden), BF16),
            pltpu.VMEM((L, W, s.hidden), BF16),
            pltpu.VMEM((s.down_slots, L, FC, W), BF16),
            pltpu.VMEM((C, 3, R, FC), BF16),
            pltpu.VMEM((C, 3, R, FC), BF16),
            pltpu.VMEM((C, 3, R, FC), BF16),
            pltpu.VMEM((C, 3, R, FC), BF16),
            pltpu.VMEM((3, 3, s.unit_rows, FC), F32),
            pltpu.VMEM((R, W), F32),
            pltpu.VMEM((n, E, T2, 2, held, W), BF16),
            pltpu.VMEM((n, E, T2, held, W), BF16),
            pltpu.VMEM((n, E, T2, held, W), BF16),
            pltpu.VMEM((M, n, held, W), BF16),
            pltpu.VMEM((n, held, W), BF16),
            dma((C,)),
            dma((n,)), dma((n,)),
            dma, dma,
            dma((n,)), dma((n,)),
            dma((n,)), dma((n,)),
            dma, dma((U * s.subs,)), dma((U * s.subs,)), dma,
            dma, dma,
            dma, dma((n,)),
            dma((n,)), dma((n,)),
            dma((3,)), dma, dma((5,)),
        ],
        compiler_params=pltpu.CompilerParams(
            collective_id=0, has_side_effects=True, vmem_limit_bytes=67_043_328),
        name="exchange",
    )(*args)


def grads_kernel(s, tokens_in, x_hbm, g_hbm, res_hbm, tokens_out, gate_hbm, up_hbm, down_hbm,
                 tokens, x, g, res, gate, up, down, xsem, rsem, wsem):
    C, FC = s.chunks, s.cols
    x_load = pltpu.make_async_copy(x_hbm, x, xsem.at[0])
    g_load = pltpu.make_async_copy(g_hbm, g, xsem.at[1])

    def res_load(c):
        return pltpu.make_async_copy(res_hbm.at[c], res.at[c], rsem.at[c])

    x_load.start()
    res_load(0).start()
    g_load.start()
    tokens_load = pltpu.make_async_copy(tokens_in, tokens, xsem.at[2])
    tokens_store = pltpu.make_async_copy(tokens, tokens_out, xsem.at[2])

    def stores(c, slot):
        columns = pl.ds(pl.multiple_of(c * FC, FC), FC)
        return (
            pltpu.make_async_copy(gate.at[slot], gate_hbm.at[:, :, columns], wsem.at[slot, 0]),
            pltpu.make_async_copy(up.at[slot], up_hbm.at[:, :, columns], wsem.at[slot, 1]),
            pltpu.make_async_copy(down.at[slot], down_hbm.at[:, columns, :], wsem.at[slot, 2]),
        )

    x_load.wait()
    for c in range(1, C):
        res_load(c).start()
    tokens_load.start()

    def step(c, carry):
        slot = lax.rem(c, 2)
        out = stores(c, slot)
        res_load(c).wait()
        for i, buffer in ((1, gate), (2, up), (0, down)):
            @pl.when(c >= 2)
            def _():
                out[(i + 2) % 3].wait()

            if i == 0:
                @pl.when(c == 0)
                def _():
                    g_load.wait()

            for l in range(s.local):
                rows = pl.ds(l * s.rows, s.rows)
                left, right = (res[c, 0, rows, :], g[rows, :]) if i == 0 else (x[rows, :], res[c, i, rows, :])
                buffer[slot, l] = lax.dot_general(left, right, TN, preferred_element_type=F32).astype(BF16)
            out[(i + 2) % 3].start()
        return carry

    lax.fori_loop(0, C, step, 0)
    tokens_load.wait()
    tokens_store.start()
    for c in range(max(C - 2, 0), C):
        for copy in stores(c, c % 2):
            copy.wait()
    tokens_store.wait()


def weight_grads(s, token_grad, x, g, res):
    W, FC, R, C, L = s.slice, s.cols, s.all_rows, s.chunks, s.local
    anywhere = pl.BlockSpec(memory_space=pl.ANY)
    dma = pltpu.SemaphoreType.DMA
    return pl.pallas_call(
        functools.partial(grads_kernel, s),
        out_shape=(
            jax.ShapeDtypeStruct((s.held, s.width), BF16),
            jax.ShapeDtypeStruct((L, W, s.hidden), BF16),
            jax.ShapeDtypeStruct((L, W, s.hidden), BF16),
            jax.ShapeDtypeStruct((L, s.hidden, W), BF16),
        ),
        in_specs=[anywhere] * 4,
        out_specs=(anywhere,) * 4,
        scratch_shapes=[
            pltpu.VMEM((s.held, s.width), BF16),
            pltpu.VMEM((R, W), BF16),
            pltpu.VMEM((R, W), BF16),
            pltpu.VMEM((C, 3, R, FC), BF16),
            pltpu.VMEM((2, L, W, FC), BF16),
            pltpu.VMEM((2, L, W, FC), BF16),
            pltpu.VMEM((2, L, FC, W), BF16),
            dma((3,)), dma((C,)), dma((2, 3)),
        ],
        name="weight_grads",
    )(token_grad, x, g, res)


def shards(tokens, out_grad, route_probs, expert_ids, slot_index, w_gate, w_up, w_down):
    n, e, t = (lax.axis_size(a) for a in ("dp", "expert", "tensor"))
    held, width = tokens.shape
    s = Sizes(n, e, t, held, width, w_gate.shape[0], w_gate.shape[2])
    token_grad, x, g, res = exchange(
        s, tokens, out_grad, route_probs.T, expert_ids.T, slot_index.T, w_gate, w_up, w_down)
    return weight_grads(s, token_grad, x, g, res)


def solution(mesh):
    placed = (
        P(("dp", "expert", "tensor"), None),
        P(("dp", "expert", "tensor"), None),
        P(("dp", "expert"), None),
        P(("dp", "expert"), None),
        P(("dp", "expert"), None),
        P("expert", "dp", "tensor"),
        P("expert", "dp", "tensor"),
        P("expert", "tensor", "dp"),
    )
    return jax.shard_map(
        shards,
        mesh=mesh,
        in_specs=placed,
        out_specs=(
            P(("dp", "expert", "tensor"), None),
            P("expert", "dp", "tensor"),
            P("expert", "dp", "tensor"),
            P("expert", "tensor", "dp"),
        ),
        check_vma=False,
    )
```

time: 149 us -> 133 us (0.89)
  Pallas kernels: 143 us -> 132 us
  other arithmetic: 2.72 us -> 0 us
  local copies, waits for them, and re-layouts: 1.8 us -> 0 us
    pallas_call x1, Pallas kernels: 123 us -> 114 us  [exchange(): pl.pallas_call(functools.partial(exchange_kernel, s), out_shape=(jax.Shap...]
    pallas_call x1, Pallas kernels: 20 us -> 18.3 us  [weight_grads(): pl.pallas_call(functools.partial(grads_kernel, s), out_shape=(jax.ShapeDt...]
where the time goes in v2:
time: 133 us
  Pallas kernels  132 us (99%)
    pallas_call x1, Pallas kernels, exchange(): pl.pallas_call(functools.partial(exchange_kernel, s), out_shape=(jax.Shap...  114 us
    pallas_call x1, Pallas kernels, weight_grads(): pl.pallas_call(functools.partial(grads_kernel, s), out_shape=(jax.ShapeDt...  18.3 us

profile of v2, /device:TPU:0, one launch (start us, length us, event | category | flops | bytes accessed | tf_op | source)
XLA Modules:
  0.0 132.8 jit_solution(9988327922881978421)
XLA Ops:
  0.6 113.9 %exchange.1 = (bf16[8,4096]{1,0:T(8,128)(2,1)}, bf16[320,1024]{1,0:T(8,128)(2,1)}, bf16[320,1024]{1,0:T(8,128)(2,1)}, bf16[7,3,320,256]{3,2,1,0:T(8,128)(2,1)}) custom-call(bf16[8,4096]{1,0:T(8,128)(2,1)} %tok_hbm.1, bf16[8,4096]{1,0:T(8,128)(2,1)} %dout_hbm.1, f32[2,32]{1,0:T(2,128)} %bitcast.3, s32[2,32]{1,0:T(2,128)} %bitcast.4, s32[2,32]{1,0:T(2,128)} %bitcast.5, ...), custom_call_target="tpu_custom_call" | custom-call | tf_op jit(solution)/shard_map/exchange/pallas_call | solution.py:483
  114.5 18.3 %weight_grads.1 = (bf16[8,4096]{1,0:T(8,128)(2,1)}, bf16[4,1024,1792]{2,1,0:T(8,128)(2,1)}, bf16[4,1024,1792]{2,1,0:T(8,128)(2,1)}, bf16[4,1792,1024]{2,1,0:T(8,128)(2,1)}) custom-call(bf16[8,4096]{1,0:T(8,128)(2,1)} %get-tuple-element.8.tokens_in, bf16[320,1024]{1,0:T(8,128)(2,1)} %get-tuple-element.9.x_hbm, bf16[320,1024]{1,0:T(8,128)(2,1)} %get-tuple-element.10.g_hbm, ...), custom_call_target="tpu_custom_call" | custom-call | tf_op jit(solution)/shard_map/weight_grads/pallas_call | solution.py:600

commit v3 on v2

--- a/solution.py
+++ b/solution.py
@@ -38,7 +38,7 @@
         self.per_unit = max(local // self.cuts, 1)
         self.part_rows = self.unit_rows // self.per_unit
         self.units = self.cuts * self.chunks
-        self.subs = self.cols // 128
+        self.subs = 1
         self.down_slots = min(4, self.chunks)
 
 
@@ -239,7 +239,7 @@
     def piece(ref, u, b):
         c, h = unit(u)
         rows = pl.ds(pl.multiple_of(h * s.unit_rows, s.unit_rows), s.unit_rows)
-        return ref.at[c, :, rows, pl.ds(b * 128, 128)]
+        return ref.at[c, :, rows, pl.ds(0, s.cols)]
 
     def expert_of(h, j):
         return h * s.per_unit + j if s.local >= s.cuts else h * s.local // s.cuts
@@ -338,7 +338,7 @@
 
             for b in range(s.subs):
                 from_outer(u, b).wait_recv()
-                columns = pl.ds(b * 128, 128)
+                columns = pl.ds(0, s.cols)
 
                 def add(r):
                     here = pl.ds(r, tile)
@@ -356,7 +356,7 @@
             c, h = unit(u)
             for b in range(s.subs):
                 to_across(u, b).wait_recv()
-                columns = pl.ds(b * 128, 128)
+                columns = pl.ds(0, s.cols)
 
                 def act(r):
                     here = pl.ds(r, tile)
@@ -408,35 +408,38 @@
                 lo = (2 * j + p) * s.held
                 tp[at[0], at[1], at[2], p] = out[lo : lo + s.held].astype(BF16)
 
-    loop(0, s.tokens // span, combine)
-    pair_copy = remote(tp.at[:, :, :, 1 - par], pair_in, es, er, other)
-    pair_copy.start()
-    pair_copy.wait_recv()
+    def pair_copy(i):
+        half = pl.ds(i * (n // 2), n // 2)
+        return remote(tp.at[half, :, :, 1 - par], pair_in.at[half], es.at[i], er.at[i], other)
 
     def pair_sum(i):
         at = (i // s.plane, lax.rem(i, s.plane) // s.pairs, lax.rem(i, s.pairs))
         v = tp[at[0], at[1], at[2], par].astype(F32) + pair_in[at].astype(F32)
         sum_a[at] = v.astype(BF16)
 
-    loop(0, n * s.plane, pair_sum)
-
-    def plane_copy(d, k):
-        q, to = lax.rem(spot + k, s.plane), lax.rem(z + d, n)
-        return remote(sum_a.at[to, q // s.pairs, lax.rem(q, s.pairs)], plane_in.at[k, to], fs, fr.at[d],
+    def plane_copy(to, k):
+        q = lax.rem(spot + k, s.plane)
+        return remote(sum_a.at[to, q // s.pairs, lax.rem(q, s.pairs)], plane_in.at[k, to], fs, fr.at[to],
                       plane_dev(q))
 
-    ranks = [n // 2] + [d for d in range(1, n) if d != n // 2] + [0]
-    for d in ranks:
-        loop(1, s.plane, lambda k: plane_copy(d, k).start())
+    spans = s.tokens // span
+    for i in range(2):
+        loop(i * (spans // 2), (i + 1) * (spans // 2), combine)
+        pair_copy(i).start()
+    for i in range(2):
+        pair_copy(i).wait_recv()
+        loop(i * (n * s.plane // 2), (i + 1) * (n * s.plane // 2), pair_sum)
+        for to in range(i * (n // 2), (i + 1) * (n // 2)):
+            loop(1, s.plane, lambda k: plane_copy(to, k).start())
     all_in = plane_in.at[pl.ds(1, s.plane - 1)]
     sums = remote(all_in, all_in, fs, fr.at[0], plane_dev(lax.rem(spot + 1, s.plane)))
 
-    def last(d):
-        to = lax.rem(z + d, n)
+    def last(to):
         one_in = plane_in.at[pl.ds(1, s.plane - 1), to]
-        remote(one_in, one_in, fs, fr.at[d], plane_dev(lax.rem(spot + 1, s.plane))).wait_recv()
+        remote(one_in, one_in, fs, fr.at[to], plane_dev(lax.rem(spot + 1, s.plane))).wait_recv()
         v = sum_a[to, e, t2].astype(F32)
-        return to, lax.fori_loop(1, s.plane, lambda k, a: a + plane_in[k, to].astype(F32), v).astype(BF16)
+        v = lax.fori_loop(1, s.plane, lambda k, a: a + plane_in[k, to].astype(F32), v)
+        sum_b[to] = v.astype(BF16)
 
     def final_copy(d):
         to = lax.rem(z + d, n)
@@ -448,12 +451,13 @@
         return remote(sum_b.at[frm], token_grad.at[:, pl.ds(pl.multiple_of(frm * W, W), W)], hs.at[d], hr.at[d],
                       {"dp": frm})
 
-    for d in ranks[:-1]:
-        to, v = last(d)
-        sum_b[to] = v
-        final_copy(d).start()
-    _, v = last(0)
-    sum_b[z] = v
+    for to in range(n):
+        last(to)
+
+        @pl.when(z != to)
+        def _():
+            final_copy(lax.rem(to + n - z, n)).start()
+
     own_out = pltpu.make_async_copy(
         sum_b.at[z], token_grad.at[:, pl.ds(pl.multiple_of(z * W, W), W)], osem.at[2])
     own_out.start()
@@ -464,7 +468,8 @@
         all_plane(d).wait_send()
         core_copy(d).wait_send()
     all_routes().wait_send()
-    pair_copy.wait_send()
+    for i in range(2):
+        pair_copy(i).wait_send()
     sums.wait_send()
     x_copy.wait()
     g_copy.wait()
@@ -524,7 +529,7 @@
             dma((n,)), dma((n,)),
             dma((n,)), dma((n,)),
             dma, dma((U * s.subs,)), dma((U * s.subs,)), dma,
-            dma, dma,
+            dma((2,)), dma((2,)),
             dma, dma((n,)),
             dma((n,)), dma((n,)),
             dma((3,)), dma, dma((5,)),
@@ -551,7 +556,7 @@
     tokens_store = pltpu.make_async_copy(tokens, tokens_out, xsem.at[2])
 
     def stores(c, slot):
-        columns = pl.ds(pl.multiple_of(c * FC, FC), FC)
+        columns = pl.ds(c * FC, FC)
         return (
             pltpu.make_async_copy(gate.at[slot], gate_hbm.at[:, :, columns], wsem.at[slot, 0]),
             pltpu.make_async_copy(up.at[slot], up_hbm.at[:, :, columns], wsem.at[slot, 1]),
@@ -564,18 +569,14 @@
     tokens_load.start()
 
     def step(c, carry):
-        slot = lax.rem(c, 2)
+        slot = c % 2
         out = stores(c, slot)
         res_load(c).wait()
         for i, buffer in ((1, gate), (2, up), (0, down)):
-            @pl.when(c >= 2)
-            def _():
+            if c >= 2:
                 out[(i + 2) % 3].wait()
-
-            if i == 0:
-                @pl.when(c == 0)
-                def _():
-                    g_load.wait()
+            if i == 0 and c == 0:
+                g_load.wait()
 
             for l in range(s.local):
                 rows = pl.ds(l * s.rows, s.rows)
@@ -584,7 +585,8 @@
             out[(i + 2) % 3].start()
         return carry
 
-    lax.fori_loop(0, C, step, 0)
+    for c in range(C):
+        step(c, 0)
     tokens_load.wait()
     tokens_store.start()
     for c in range(max(C - 2, 0), C):

time: 133 us -> 131 us (0.985)
  Pallas kernels: 132 us -> 130 us
where the time goes in v3:
time: 131 us
  Pallas kernels  130 us (99%)
    pallas_call x1, Pallas kernels, exchange(): pl.pallas_call(functools.partial(exchange_kernel, s), out_shape=(jax.Shap...  113 us
    pallas_call x1, Pallas kernels, weight_grads(): pl.pallas_call(functools.partial(grads_kernel, s), out_shape=(jax.ShapeDt...  17.7 us

profile of v3, /device:TPU:0, one launch (start us, length us, event | category | flops | bytes accessed | tf_op | source)
XLA Modules:
  0.0 131.1 jit_solution(10867453423187960125)
XLA Ops:
  0.6 112.6 %exchange.1 = (bf16[8,4096]{1,0:T(8,128)(2,1)}, bf16[320,1024]{1,0:T(8,128)(2,1)}, bf16[320,1024]{1,0:T(8,128)(2,1)}, bf16[7,3,320,256]{3,2,1,0:T(8,128)(2,1)}) custom-call(bf16[8,4096]{1,0:T(8,128)(2,1)} %tok_hbm.1, bf16[8,4096]{1,0:T(8,128)(2,1)} %dout_hbm.1, f32[2,32]{1,0:T(2,128)} %bitcast.3, s32[2,32]{1,0:T(2,128)} %bitcast.4, s32[2,32]{1,0:T(2,128)} %bitcast.5, ...), custom_call_target="tpu_custom_call" | custom-call | tf_op jit(solution)/shard_map/exchange/pallas_call | solution.py:488
  113.3 17.7 %weight_grads.1 = (bf16[8,4096]{1,0:T(8,128)(2,1)}, bf16[4,1024,1792]{2,1,0:T(8,128)(2,1)}, bf16[4,1024,1792]{2,1,0:T(8,128)(2,1)}, bf16[4,1792,1024]{2,1,0:T(8,128)(2,1)}) custom-call(bf16[8,4096]{1,0:T(8,128)(2,1)} %get-tuple-element.8.tokens_in, bf16[320,1024]{1,0:T(8,128)(2,1)} %get-tuple-element.9.x_hbm, bf16[320,1024]{1,0:T(8,128)(2,1)} %get-tuple-element.10.g_hbm, ...), custom_call_target="tpu_custom_call" | custom-call | tf_op jit(solution)/shard_map/weight_grads/pallas_call | solution.py:602

commit v4 on v3

--- a/solution.py
+++ b/solution.py
@@ -563,6 +563,13 @@
             pltpu.make_async_copy(down.at[slot], down_hbm.at[:, columns, :], wsem.at[slot, 2]),
         )
 
+    def one_store(i, c, slot, l):
+        columns = pl.ds(c * FC, FC)
+        if i == 0:
+            return pltpu.make_async_copy(down.at[slot, l], down_hbm.at[l, columns, :], wsem.at[slot, 2])
+        a, b = ((gate, gate_hbm), (up, up_hbm))[i - 1]
+        return pltpu.make_async_copy(a.at[slot, l], b.at[l, :, columns], wsem.at[slot, i - 1])
+
     x_load.wait()
     for c in range(1, C):
         res_load(c).start()
@@ -582,7 +589,10 @@
                 rows = pl.ds(l * s.rows, s.rows)
                 left, right = (res[c, 0, rows, :], g[rows, :]) if i == 0 else (x[rows, :], res[c, i, rows, :])
                 buffer[slot, l] = lax.dot_general(left, right, TN, preferred_element_type=F32).astype(BF16)
-            out[(i + 2) % 3].start()
+                if c == 0 or c == C - 1:
+                    one_store(i, c, slot, l).start()
+            if c != 0 and c != C - 1:
+                out[(i + 2) % 3].start()
         return carry
 
     for c in range(C):

time: 131 us -> 131 us (level)
  no operation moved by 1% of the time
where the time goes in v4:
time: 131 us
  Pallas kernels  130 us (99%)
    pallas_call x1, Pallas kernels, exchange(): pl.pallas_call(functools.partial(exchange_kernel, s), out_shape=(jax.Shap...  113 us
    pallas_call x1, Pallas kernels, weight_grads(): pl.pallas_call(functools.partial(grads_kernel, s), out_shape=(jax.ShapeDt...  17.6 us

profile of v4, /device:TPU:0, one launch (start us, length us, event | category | flops | bytes accessed | tf_op | source)
XLA Modules:
  0.0 131.1 jit_solution(11093086860927197725)
XLA Ops:
  0.6 112.6 %exchange.1 = (bf16[8,4096]{1,0:T(8,128)(2,1)}, bf16[320,1024]{1,0:T(8,128)(2,1)}, bf16[320,1024]{1,0:T(8,128)(2,1)}, bf16[7,3,320,256]{3,2,1,0:T(8,128)(2,1)}) custom-call(bf16[8,4096]{1,0:T(8,128)(2,1)} %tok_hbm.1, bf16[8,4096]{1,0:T(8,128)(2,1)} %dout_hbm.1, f32[2,32]{1,0:T(2,128)} %bitcast.3, s32[2,32]{1,0:T(2,128)} %bitcast.4, s32[2,32]{1,0:T(2,128)} %bitcast.5, ...), custom_call_target="tpu_custom_call" | custom-call | tf_op jit(solution)/shard_map/exchange/pallas_call | solution.py:488
  113.3 17.6 %weight_grads.1 = (bf16[8,4096]{1,0:T(8,128)(2,1)}, bf16[4,1024,1792]{2,1,0:T(8,128)(2,1)}, bf16[4,1024,1792]{2,1,0:T(8,128)(2,1)}, bf16[4,1792,1024]{2,1,0:T(8,128)(2,1)}) custom-call(bf16[8,4096]{1,0:T(8,128)(2,1)} %get-tuple-element.8.tokens_in, bf16[320,1024]{1,0:T(8,128)(2,1)} %get-tuple-element.9.x_hbm, bf16[320,1024]{1,0:T(8,128)(2,1)} %get-tuple-element.10.g_hbm, ...), custom_call_target="tpu_custom_call" | custom-call | tf_op jit(solution)/shard_map/weight_grads/pallas_call | solution.py:612
